TPU v7x, 32 devices: a whole 2x2x4 slice. The times are simulated.
32 devices in a mesh: rows: 8 (over z, x), cols: 4 (over y, core).
Axes of the slice: x: 2, y: 2, z: 4, core: 2. Of those that a mesh axis runs over, the one named last changes fastest.
Arguments:
- coupling: float32 [2, 16384, 16384], P(None, 'rows', 'cols'), may hold values from -2 to 40, as said below
- initial: float32 [2, 48, 16384], P(None, None, 'rows'), may hold values from -8 to 8
Outputs:
- basis: float32 [2, 48, 16384], P(None, None, ('rows', 'cols'))
- ritz: float32 [4, 2, 48, 48], replicated
Inputs may be any that keep to these rules, and one draw needn't show every extreme that they name: `coupling`: H is Hermitian (the first plane symmetric, the second antisymmetric) and positive definite.
All inputs are finite; a program needn't handle non-finite values.
Results may differ from a plain program's by a relative error of at most 0.0003.
Values sent between devices are 32-bit elements; how exact they have to be, the bound alone decides.
No kernel may reach another device: no remote copies, remote signals or barrier semaphores. Data moves between devices by JAX's collectives and lax.ppermute only.
A program may use at most 128 MiB of HBM per device.

v0:
```python
import jax
import jax.numpy as jnp
from jax import lax
from jax.sharding import PartitionSpec as P

N = 16384
ITERS = 4
HIGH = lax.Precision.HIGHEST


def pair_products(left, right):
    real_part = jnp.dot(left[0], right[0].T, precision=HIGH) + jnp.dot(
        left[1], right[1].T, precision=HIGH
    )
    imag_part = jnp.dot(left[0], right[1].T, precision=HIGH) - jnp.dot(
        left[1], right[0].T, precision=HIGH
    )
    return jnp.stack([real_part, imag_part])


def orthonormal(gram_matrix, images):
    gram_re = gram_matrix[0]
    gram_im = gram_matrix[1]
    vectors = gram_re.shape[0]
    width = images.shape[2]
    upper_pair = jnp.stack([gram_re, -gram_im], axis=-1)
    lower_pair = jnp.stack([gram_im, gram_re], axis=-1)
    embedded = jnp.stack([upper_pair, lower_pair], axis=1).reshape(2 * vectors, 2 * vectors)
    factor = jnp.linalg.cholesky(embedded)
    woven = jnp.transpose(images, (1, 0, 2)).reshape(2 * vectors, width)
    solved = lax.linalg.triangular_solve(factor, woven, left_side=True, lower=True)
    return jnp.transpose(solved.reshape(vectors, 2, width), (1, 0, 2))


def tile_product(coupling, local_block):
    vectors = local_block.shape[1]
    stacked = local_block.reshape(2 * vectors, local_block.shape[2])
    contract = (((1,), (1,)), ((), ()))
    with_real = lax.dot_general(
        stacked, coupling[0], contract, precision=HIGH, preferred_element_type=jnp.float32
    )
    with_imag = lax.dot_general(
        stacked, coupling[1], contract, precision=HIGH, preferred_element_type=jnp.float32
    )
    return jnp.stack(
        [with_real[:vectors] - with_imag[vectors:], with_real[vectors:] + with_imag[:vectors]]
    )


def body(coupling, initial):
    row_width = initial.shape[2]
    per_column = lax.axis_size("rows") // lax.axis_size("cols")
    column = lax.axis_index("cols")
    block_span = row_width * per_column
    piece_width = row_width // lax.axis_size("cols")
    order_value = float(N)
    ritz_list = []
    current = lax.dynamic_slice_in_dim(initial, column * piece_width, piece_width, 2)
    for iteration in range(ITERS):
        gathered = lax.all_gather(current, ("rows", "cols"), axis=2, tiled=True)
        local_block = lax.dynamic_slice_in_dim(gathered, column * block_span, block_span, 2)
        partial_value = tile_product(coupling, local_block)
        images = lax.psum_scatter(partial_value, "cols", scatter_dimension=2, tiled=True)
        gram_matrix, projection = lax.psum(
            (pair_products(images, images), pair_products(current, images)), ("rows", "cols")
        )
        ritz_list.append(projection / order_value)
        current = orthonormal(gram_matrix / order_value, images)
    return (current, jnp.stack(ritz_list))


def solution(mesh):
    placed = (P(None, "rows", "cols"), P(None, None, "rows"))
    return jax.shard_map(
        body,
        mesh=mesh,
        in_specs=placed,
        out_specs=(P(None, None, ("rows", "cols")), P()),
        check_vma=False,
    )
```

profile of v0, /device:TPU:0, one launch (start us, length us, event | category | flops | bytes accessed | tf_op | source)
XLA Modules:
  0.0 1063.4 jit_solution(4548301341809468267)
XLA Ops:
  9.1 74.6 %all-gather.5.cloned.1.call-done = f32[2,48,16384]{2,1,0:T(8,128)} async-done(((f32[2,48,512]{2,1,0:T(8,128)}), f32[2,48,16384]{2,1,0:T(8,128)}) %all-gather.5.cloned.1.call-update) | async-done | bytes 6291472 | tf_op jit(solution)/shard_map/all_gather | solution.py:60
  83.7 1.5 constant_dynamic-slice_fusion.3
  85.2 36.0 %fusion.6 = f32[96,2048]{1,0:T(8,128)S(1)} fusion(f32[96,4096]{1,0:T(8,128)S(1)} %bitcast.280, f32[2,2048,4096]{2,1,0:T(8,128)} %param.5), kind=kOutput, calls=%fused_computation.6 | convolution fusion | flops 9663676416 | bytes 35913728 | tf_op jit(solution)/shard_map/dot_general | solution.py:42
  121.2 36.8 %fusion.14 = f32[96,2048]{1,0:T(8,128)} fusion(f32[96,4096]{1,0:T(8,128)S(1)} %bitcast.281, f32[2,2048,4096]{2,1,0:T(8,128)} %param.5), kind=kOutput, calls=%fused_computation.14 | convolution fusion | flops 9663676416 | bytes 35913728 | tf_op jit(solution)/shard_map/dot_general | solution.py:39
  158.0 1.2 fusion.47
  160.3 22.1 %reduce-scatter.5.cloned.1.call-done = f32[2,48,512]{2,1,0:T(8,128)} async-done(((f32[2,48,2048]{2,1,0:T(8,128)}), f32[2,48,512]{2,1,0:T(8,128)}) %reduce-scatter.5.cloned.1.call-update) | async-done | bytes 196624 | tf_op jit(solution)/shard_map/reduce_scatter | solution.py:63
  183.5 1.2 fusion.57
  185.9 1.2 fusion.39
  187.1 40.3 %psum.56 = f32[2,48,48]{2,1,0:T(8,128)S(1)} all-reduce(f32[2,48,48]{2,1,0:T(8,128)S(1)} %pad_maximum_fusion.9), channel_id=1, replica_groups=mesh['rows'=8,'cols'=4] {'rows','cols'}, use_global_device_ids=true, to_apply=%region_1.0 | all-reduce | flops 4608 | bytes 36864 | tf_op jit(solution)/shard_map/psum | solution.py:64
  230.7 8.8 cholesky.74
  240.8 7.4 custom-call.8
  249.4 70.3 %all-gather.7.cloned.1.call-done = f32[2,48,16384]{2,1,0:T(8,128)} async-done(((f32[2,48,512]{2,1,0:T(8,128)}), f32[2,48,16384]{2,1,0:T(8,128)}) %all-gather.7.cloned.1.call-update) | async-done | bytes 6291472 | tf_op jit(solution)/shard_map/all_gather | solution.py:60
  319.8 1.5 constant_dynamic-slice_fusion.2
  321.3 36.1 %fusion.4 = f32[96,2048]{1,0:T(8,128)S(1)} fusion(f32[96,4096]{1,0:T(8,128)S(1)} %bitcast.282, f32[2,2048,4096]{2,1,0:T(8,128)} %param.5), kind=kOutput, calls=%fused_computation.4 | convolution fusion | flops 9663676416 | bytes 35913728 | tf_op jit(solution)/shard_map/dot_general | solution.py:42
  357.4 36.7 %fusion.12 = f32[96,2048]{1,0:T(8,128)} fusion(f32[96,4096]{1,0:T(8,128)S(1)} %bitcast.283, f32[2,2048,4096]{2,1,0:T(8,128)} %param.5), kind=kOutput, calls=%fused_computation.12 | convolution fusion | flops 9663676416 | bytes 35913728 | tf_op jit(solution)/shard_map/dot_general | solution.py:39
  394.1 1.2 fusion.45
  396.4 22.1 %reduce-scatter.7.cloned.1.call-done = f32[2,48,512]{2,1,0:T(8,128)} async-done(((f32[2,48,2048]{2,1,0:T(8,128)}), f32[2,48,512]{2,1,0:T(8,128)}) %reduce-scatter.7.cloned.1.call-update) | async-done | bytes 196624 | tf_op jit(solution)/shard_map/reduce_scatter | solution.py:63
  419.6 1.2 fusion.59
  420.8 1.2 fusion.36
  422.0 1.2 fusion.37
  423.2 39.9 %psum.57 = f32[2,48,48]{2,1,0:T(8,128)S(1)} all-reduce(f32[2,48,48]{2,1,0:T(8,128)S(1)} %pad_maximum_fusion.10), channel_id=1, replica_groups=mesh['rows'=8,'cols'=4] {'rows','cols'}, use_global_device_ids=true, to_apply=%region_5.8 | all-reduce | flops 4608 | bytes 36864 | tf_op jit(solution)/shard_map/psum | solution.py:64
  466.4 8.8 cholesky.85
  476.6 7.4 custom-call.9
  485.2 70.3 %all-gather.9.cloned.1.call-done = f32[2,48,16384]{2,1,0:T(8,128)} async-done(((f32[2,48,512]{2,1,0:T(8,128)}), f32[2,48,16384]{2,1,0:T(8,128)}) %all-gather.9.cloned.1.call-update) | async-done | bytes 6291472 | tf_op jit(solution)/shard_map/all_gather | solution.py:60
  555.5 1.5 constant_dynamic-slice_fusion.1
  557.0 36.3 %fusion.2 = f32[96,2048]{1,0:T(8,128)S(1)} fusion(f32[96,4096]{1,0:T(8,128)S(1)} %bitcast.284, f32[2,2048,4096]{2,1,0:T(8,128)} %param.5), kind=kOutput, calls=%fused_computation.2 | convolution fusion | flops 9663676416 | bytes 35913728 | tf_op jit(solution)/shard_map/dot_general | solution.py:42
  593.3 37.0 %fusion.10 = f32[96,2048]{1,0:T(8,128)} fusion(f32[96,4096]{1,0:T(8,128)S(1)} %bitcast.285, f32[2,2048,4096]{2,1,0:T(8,128)} %param.5), kind=kOutput, calls=%fused_computation.10 | convolution fusion | flops 9663676416 | bytes 35913728 | tf_op jit(solution)/shard_map/dot_general | solution.py:39
  630.3 1.2 fusion.43
  632.6 22.1 %reduce-scatter.9.cloned.1.call-done = f32[2,48,512]{2,1,0:T(8,128)} async-done(((f32[2,48,2048]{2,1,0:T(8,128)}), f32[2,48,512]{2,1,0:T(8,128)}) %reduce-scatter.9.cloned.1.call-update) | async-done | bytes 196624 | tf_op jit(solution)/shard_map/reduce_scatter | solution.py:63
  655.8 1.2 fusion.61
  658.2 1.2 fusion.35
  659.4 39.9 %psum.58 = f32[2,48,48]{2,1,0:T(8,128)S(1)} all-reduce(f32[2,48,48]{2,1,0:T(8,128)S(1)} %pad_maximum_fusion.11), channel_id=1, replica_groups=mesh['rows'=8,'cols'=4] {'rows','cols'}, use_global_device_ids=true, to_apply=%region_7.10 | all-reduce | flops 4608 | bytes 36864 | tf_op jit(solution)/shard_map/psum | solution.py:64
  701.3 1.7 copy.21
  702.9 1.5 reshape.112
  706.1 8.8 cholesky.96
  716.2 7.4 custom-call.10
  726.4 68.7 %all-gather.11.cloned.1.call-done = f32[2,48,16384]{2,1,0:T(8,128)} async-done(((f32[2,48,512]{2,1,0:T(8,128)}), f32[2,48,16384]{2,1,0:T(8,128)}) %all-gather.11.cloned.1.call-update) | async-done | bytes 6291472 | tf_op jit(solution)/shard_map/all_gather | solution.py:60
  795.1 1.5 constant_dynamic-slice_fusion
  796.7 36.7 %fusion = f32[96,2048]{1,0:T(8,128)} fusion(f32[96,4096]{1,0:T(8,128)S(1)} %bitcast.278, f32[2,2048,4096]{2,1,0:T(8,128)} %param.5), kind=kOutput, calls=%fused_computation | convolution fusion | flops 9663676416 | bytes 35913728 | tf_op jit(solution)/shard_map/dot_general | solution.py:42
  833.4 36.8 %fusion.8 = f32[96,2048]{1,0:T(8,128)} fusion(f32[96,4096]{1,0:T(8,128)S(1)} %bitcast.279, f32[2,2048,4096]{2,1,0:T(8,128)} %param.5), kind=kOutput, calls=%fused_computation.8 | convolution fusion | flops 9663676416 | bytes 35913728 | tf_op jit(solution)/shard_map/dot_general | solution.py:39
  870.2 1.5 fusion.41
  876.2 18.7 %reduce-scatter.11.cloned.1.call-done = f32[2,48,512]{2,1,0:T(8,128)} async-done(((f32[2,48,2048]{2,1,0:T(8,128)}), f32[2,48,512]{2,1,0:T(8,128)}) %reduce-scatter.11.cloned.1.call-update) | async-done | bytes 196624 | tf_op jit(solution)/shard_map/reduce_scatter | solution.py:63
  901.2 1.2 fusion.63
  902.4 1.2 fusion.32
  903.6 1.2 fusion.33
  906.6 126.8 %all-reduce.3.cloned.1.call-done = (f32[2,48,48]{2,1,0:T(8,128)}, f32[2,48,48]{2,1,0:T(8,128)}, f32[2,48,48]{2,1,0:T(8,128)}, f32[2,48,48]{2,1,0:T(8,128)}, f32[2,48,48]{2,1,0:T(8,128)}) async-done(((f32[2,48,48]{2,1,0:T(8,128)}, f32[2,48,48]{2,1,0:T(8,128)}, f32[2,48,48]{2,1,0:T(8,128)}, f32[2,48,48]{2,1,0:T(8,128)}, f32[2,48,48]{2,1,0:T(8,128)}), (f32[2,48,48]{2,1,0:T(8,128)}, f32[2,48,48]{2,1,0:T(8,128)}, ...) | async-done | bytes 92176 | tf_op jit(solution)/shard_map/psum | solution.py:64
  1036.3 8.8 cholesky.107
  1046.4 7.4 custom-call.11
  (140 shorter events, 49.4 us)
Async XLA Ops:
  7.2 1.1 copy-start
  7.2 76.5 %all-gather.5.cloned.1.call-start = ((), (), s32[]{:S(2)}) async-start(), calls=%async_computation.4 | async-start | bytes 6488064 | tf_op jit(solution)/shard_map/all_gather | solution.py:60
  9.0 173.3 %reduce-scatter.5.cloned.1.call-start = ((), (), s32[]{:S(2)}) async-start(), calls=%async_computation.5 | async-start | bytes 983040 | tf_op jit(solution)/shard_map/reduce_scatter | solution.py:63
  160.2 159.5 %all-gather.7.cloned.1.call-start = ((), (), s32[]{:S(2)}) async-start(), calls=%async_computation.6 | async-start | bytes 6488064 | tf_op jit(solution)/shard_map/all_gather | solution.py:60
  249.4 169.1 %reduce-scatter.7.cloned.1.call-start = ((), (), s32[]{:S(2)}) async-start(), calls=%async_computation.7 | async-start | bytes 983040 | tf_op jit(solution)/shard_map/reduce_scatter | solution.py:63
  396.3 159.2 %all-gather.9.cloned.1.call-start = ((), (), s32[]{:S(2)}) async-start(), calls=%async_computation.8 | async-start | bytes 6488064 | tf_op jit(solution)/shard_map/all_gather | solution.py:60
  485.2 169.5 %reduce-scatter.9.cloned.1.call-start = ((), (), s32[]{:S(2)}) async-start(), calls=%async_computation.9 | async-start | bytes 983040 | tf_op jit(solution)/shard_map/reduce_scatter | solution.py:63
  631.5 93.3 %copy-start.1 = (f32[2,48,512]{2,1,0:T(8,128)S(1)}, f32[2,48,512]{2,1,0:T(8,128)}, u32[]{:S(2)}) copy-start(f32[2,48,512]{2,1,0:T(8,128)} %reduce-scatter.5.cloned.1.call-done) | copy-start | bytes 589828
  632.5 162.6 %all-gather.11.cloned.1.call-start = ((), (), s32[]{:S(2)}) async-start(), calls=%async_computation.10 | async-start | bytes 6488064 | tf_op jit(solution)/shard_map/all_gather | solution.py:60
  724.8 170.0 %reduce-scatter.11.cloned.1.call-start = ((), (), s32[]{:S(2)}) async-start(), calls=%async_computation.11 | async-start | bytes 983040 | tf_op jit(solution)/shard_map/reduce_scatter | solution.py:63
  833.4 39.7 %copy-start.2 = (f32[2,48,512]{2,1,0:T(8,128)S(1)}, f32[2,48,512]{2,1,0:T(8,128)}, u32[]{:S(2)}) copy-start(f32[2,48,512]{2,1,0:T(8,128)} %reduce-scatter.7.cloned.1.call-done) | copy-start | bytes 589828
  833.4 39.7 %copy-start.4 = (f32[48,2,512]{2,0,1:T(8,128)S(1)}, f32[48,2,512]{2,0,1:T(8,128)}, u32[]{:S(2)}) copy-start(f32[48,2,512]{2,0,1:T(8,128)} %copy.36) | copy-start | bytes 589828
  833.4 41.3 %copy-start.3 = (f32[2,48,512]{2,1,0:T(8,128)S(1)}, f32[2,48,512]{2,1,0:T(8,128)}, u32[]{:S(2)}) copy-start(f32[2,48,512]{2,1,0:T(8,128)} %reduce-scatter.9.cloned.1.call-done) | copy-start | bytes 589828
  833.4 41.3 %copy-start.5 = (f32[48,2,512]{2,0,1:T(8,128)S(1)}, f32[48,2,512]{2,0,1:T(8,128)}, u32[]{:S(2)}) copy-start(f32[48,2,512]{2,0,1:T(8,128)} %copy.35) | copy-start | bytes 589828
  870.2 24.6 %copy-start.6 = (f32[48,2,512]{2,0,1:T(8,128)S(1)}, f32[48,2,512]{2,0,1:T(8,128)}, u32[]{:S(2)}) copy-start(f32[48,2,512]{2,0,1:T(8,128)} %copy.34) | copy-start | bytes 589828
  872.7 160.8 %all-reduce.3.cloned.1.call-start = ((), (), s32[]{:S(2)}) async-start(), calls=%async_computation.12 | async-start | bytes 491520 | tf_op jit(solution)/shard_map/psum | solution.py:64
  1033.5 22.3 %copy-start.7 = (f32[2,48,48]{2,1,0:T(8,128)S(1)}, f32[2,48,48]{2,1,0:T(8,128)}, u32[]{:S(2)}) copy-start(f32[2,48,48]{2,1,0:T(8,128)} %get-tuple-element.7) | copy-start | bytes 55300
  1033.5 22.4 %copy-start.8 = (f32[2,48,48]{2,1,0:T(8,128)S(1)}, f32[2,48,48]{2,1,0:T(8,128)}, u32[]{:S(2)}) copy-start(f32[2,48,48]{2,1,0:T(8,128)} %get-tuple-element.8) | copy-start | bytes 55300
Sparse Core Ops, SparseCore 0:
  11.5 72.1 all-gather.4
  160.3 21.9 reduce-scatter.4
  249.5 70.1 all-gather.6
  396.4 21.9 reduce-scatter.6
  485.3 70.2 all-gather.8
  632.6 21.9 reduce-scatter.8
  724.9 70.1 all-gather.10
  872.8 21.9 reduce-scatter.10
  905.5 127.9 all-reduce.2
where the time goes:
time: 1070 us; the launch traced here: 1060 us
  waiting for transfers between devices  496 us (46%)
  matrix products  320 us (30%)
  blocking collectives  120 us (11%)
  other arithmetic  85.8 us (8%)
  local copies, waits for them, and re-layouts  25.8 us (2%)
  between operations  14.9 us (1%)
    all_gather x4, waiting for transfers between devices, body(): gathered = lax.all_gather(current, ('rows', 'cols'), axis=2, tiled=True)  284 us
    dot_general x4, matrix products, tile_product(): lax.dot_general(stacked, coupling[0], contract, precision=HIGH, preferred...  147 us
    dot_general x4, matrix products, tile_product(): lax.dot_general(stacked, coupling[1], contract, precision=HIGH, preferred...  145 us
    psum x1, waiting for transfers between devices, body(): lax.psum((pair_products(images, images), pair_products(current, images)),...  127 us
    psum x3, blocking collectives, body(): lax.psum((pair_products(images, images), pair_products(current, images)),...  120 us
    reduce_scatter x4, waiting for transfers between devices, body(): lax.psum_scatter(partial_value, 'cols', scatter_dimension=2, tiled=True)  85 us
    another operation x12, other arithmetic, orthonormal(): factor = jnp.linalg.cholesky(embedded)  37.9 us
    another operation x8, other arithmetic, orthonormal(): lax.linalg.triangular_solve(factor, woven, left_side=True, lower=True)  32 us
  transfers between devices with their start and end apart: 9, of which 9 were waited for; matrix products, arithmetic and copies ran while one was open for 1% of the time, Pallas kernels for 0%

commit v1 on v0

--- a/solution.py
+++ b/solution.py
@@ -1,3 +1,4 @@
+import functools
 import jax
 import jax.numpy as jnp
 from jax import lax
@@ -6,6 +7,21 @@
 N = 16384
 ITERS = 4
 HIGH = lax.Precision.HIGHEST
+
+
+def _perform_steps_all(in_array, array_axis):
+    return jnp.concatenate(
+        jax.lax.all_to_all(
+            jnp.stack([in_array for _ in range(jax.lax.axis_size(("rows", "cols")))], 0),
+            ("rows", "cols"),
+            0,
+            0,
+        ),
+        array_axis,
+    )
+
+
+mark_region = functools.partial(_perform_steps_all, array_axis=2)
 
 
 def pair_products(left, right):
@@ -57,7 +73,7 @@
     ritz_list = []
     current = lax.dynamic_slice_in_dim(initial, column * piece_width, piece_width, 2)
     for iteration in range(ITERS):
-        gathered = lax.all_gather(current, ("rows", "cols"), axis=2, tiled=True)
+        gathered = mark_region(current)
         local_block = lax.dynamic_slice_in_dim(gathered, column * block_span, block_span, 2)
         partial_value = tile_product(coupling, local_block)
         images = lax.psum_scatter(partial_value, "cols", scatter_dimension=2, tiled=True)

time: 1070 us -> 1380 us (1.29)
  blocking collectives: 120 us -> 408 us
  local copies, waits for them, and re-layouts: 25.8 us -> 39.9 us
    all_to_all x0 -> x2, blocking collectives: none -> 288 us  [_perform_steps_all(): jax.lax.all_to_all(jnp.stack([in_array for _ in range(jax.lax.axis_size((...]
    all_gather x4 -> x0, waiting for transfers between devices: 284 us -> none  [body(): gathered = lax.all_gather(current, ('rows', 'cols'), axis=2, tiled=True)]
    all_to_all x0 -> x2, waiting for transfers between devices: none -> 276 us  [_perform_steps_all(): jax.lax.all_to_all(jnp.stack([in_array for _ in range(jax.lax.axis_size((...]
  transfers between devices with their start and end apart: 9 -> 7, of which waited for: 9 -> 7; matrix products, arithmetic and copies ran while one was open for 1% -> 1% of each run, Pallas kernels for 0% -> 0%
where the time goes in v1:
time: 1380 us
  waiting for transfers between devices  490 us (36%)
  blocking collectives  408 us (30%)
  matrix products  322 us (23%)
  other arithmetic  87 us (6%)
  local copies, waits for them, and re-layouts  39.9 us (3%)
  between operations  15.2 us (1%)
    all_to_all x2, blocking collectives, _perform_steps_all(): jax.lax.all_to_all(jnp.stack([in_array for _ in range(jax.lax.axis_size((...  288 us
    all_to_all x2, waiting for transfers between devices, _perform_steps_all(): jax.lax.all_to_all(jnp.stack([in_array for _ in range(jax.lax.axis_size((...  276 us
    dot_general x4, matrix products, tile_product(): lax.dot_general(stacked, coupling[0], contract, precision=HIGH, preferred...  147 us
    dot_general x4, matrix products, tile_product(): lax.dot_general(stacked, coupling[1], contract, precision=HIGH, preferred...  144 us
    psum x1, waiting for transfers between devices, body(): lax.psum((pair_products(images, images), pair_products(current, images)),...  127 us
    psum x3, blocking collectives, body(): lax.psum((pair_products(images, images), pair_products(current, images)),...  120 us
    reduce_scatter x4, waiting for transfers between devices, body(): lax.psum_scatter(partial_value, 'cols', scatter_dimension=2, tiled=True)  87.7 us
    another operation x12, other arithmetic, orthonormal(): factor = jnp.linalg.cholesky(embedded)  37.8 us
  transfers between devices with their start and end apart: 7, of which 7 were waited for; matrix products, arithmetic and copies ran while one was open for 1% of the time, Pallas kernels for 0%

profile of v1, /device:TPU:0, one launch (start us, length us, event | category | flops | bytes accessed | tf_op | source)
XLA Modules:
  0.0 1375.5 jit_solution(14183722023837481648)
XLA Ops:
  8.3 3.5 stack.130
  11.8 7.4 all-to-all-start
  19.3 139.9 %all-to-all-done = f32[32,2,48,512]{3,2,1,0:T(8,128)} async-done(((f32[32,2,48,512]{3,2,1,0:T(8,128)}), f32[32,2,48,512]{3,2,1,0:T(8,128)}, u32[]{:S(2)}, u32[]{:S(2)}) %all-to-all-start) | async-done | bytes 6291488 | tf_op jit(solution)/shard_map/all_to_all | solution.py:14
  159.2 3.5 copy.58
  162.8 36.0 %fusion.6 = f32[96,2048]{1,0:T(8,128)S(1)} fusion(f32[96,4096]{1,0:T(8,128)S(1)} %bitcast.294, f32[2,2048,4096]{2,1,0:T(8,128)} %param.5), kind=kOutput, calls=%fused_computation.6 | convolution fusion | flops 9663676416 | bytes 35913728 | tf_op jit(solution)/shard_map/dot_general | solution.py:58
  198.8 36.7 %fusion.14 = f32[96,2048]{1,0:T(8,128)} fusion(f32[96,4096]{1,0:T(8,128)S(1)} %bitcast.295, f32[2,2048,4096]{2,1,0:T(8,128)} %param.5), kind=kOutput, calls=%fused_computation.14 | convolution fusion | flops 9663676416 | bytes 35913728 | tf_op jit(solution)/shard_map/dot_general | solution.py:55
  235.5 1.2 fusion.47
  237.7 24.4 %reduce-scatter.5.cloned.1.call-done = f32[2,48,512]{2,1,0:T(8,128)} async-done(((f32[2,48,2048]{2,1,0:T(8,128)}), f32[2,48,512]{2,1,0:T(8,128)}) %reduce-scatter.5.cloned.1.call-update) | async-done | bytes 196624 | tf_op jit(solution)/shard_map/reduce_scatter | solution.py:79
  263.3 1.2 fusion.81
  265.7 1.2 fusion.39
  266.9 40.0 %psum.56 = f32[2,48,48]{2,1,0:T(8,128)S(1)} all-reduce(f32[2,48,48]{2,1,0:T(8,128)S(1)} %pad_maximum_fusion.9), channel_id=1, replica_groups=mesh['rows'=8,'cols'=4] {'rows','cols'}, use_global_device_ids=true, to_apply=%region_1.0 | all-reduce | flops 4608 | bytes 36864 | tf_op jit(solution)/shard_map/psum | solution.py:80
  310.2 8.8 cholesky.74
  320.3 7.4 custom-call.8
  329.0 144.2 %all_to_all.20 = f32[32,2,48,512]{3,2,1,0:T(8,128)S(1)} all-to-all(f32[32,2,48,512]{3,2,1,0:T(8,128)S(1)} %stack.142), channel_id=1, replica_groups=mesh['rows'=8,'cols'=4] {'rows','cols'}, dimensions={0} | all-to-all | bytes 12582912 | tf_op jit(solution)/shard_map/all_to_all | solution.py:14
  474.3 36.0 %fusion.4 = f32[96,2048]{1,0:T(8,128)S(1)} fusion(f32[96,4096]{1,0:T(8,128)S(1)} %bitcast.296, f32[2,2048,4096]{2,1,0:T(8,128)} %param.5), kind=kOutput, calls=%fused_computation.4 | convolution fusion | flops 9663676416 | bytes 35913728 | tf_op jit(solution)/shard_map/dot_general | solution.py:58
  510.3 36.7 %fusion.12 = f32[96,2048]{1,0:T(8,128)} fusion(f32[96,4096]{1,0:T(8,128)S(1)} %bitcast.297, f32[2,2048,4096]{2,1,0:T(8,128)} %param.5), kind=kOutput, calls=%fused_computation.12 | convolution fusion | flops 9663676416 | bytes 35913728 | tf_op jit(solution)/shard_map/dot_general | solution.py:55
  549.2 22.4 %reduce-scatter.7.cloned.1.call-done = f32[2,48,512]{2,1,0:T(8,128)} async-done(((f32[2,48,2048]{2,1,0:T(8,128)}), f32[2,48,512]{2,1,0:T(8,128)}) %reduce-scatter.7.cloned.1.call-update) | async-done | bytes 196624 | tf_op jit(solution)/shard_map/reduce_scatter | solution.py:79
  572.8 1.2 fusion.83
  575.2 1.2 fusion.37
  576.4 39.9 %psum.57 = f32[2,48,48]{2,1,0:T(8,128)S(1)} all-reduce(f32[2,48,48]{2,1,0:T(8,128)S(1)} %pad_maximum_fusion.10), channel_id=1, replica_groups=mesh['rows'=8,'cols'=4] {'rows','cols'}, use_global_device_ids=true, to_apply=%region_5.8 | all-reduce | flops 4608 | bytes 36864 | tf_op jit(solution)/shard_map/psum | solution.py:80
  618.3 1.7 copy.38
  619.9 1.5 reshape.144
  623.1 8.8 cholesky.85
  633.2 7.4 custom-call.9
  641.9 143.9 %all_to_all.21 = f32[32,2,48,512]{3,2,1,0:T(8,128)S(1)} all-to-all(f32[32,2,48,512]{3,2,1,0:T(8,128)S(1)} %stack.154), channel_id=1, replica_groups=mesh['rows'=8,'cols'=4] {'rows','cols'}, dimensions={0} | all-to-all | bytes 12582912 | tf_op jit(solution)/shard_map/all_to_all | solution.py:14
  787.0 36.0 %fusion.2 = f32[96,2048]{1,0:T(8,128)S(1)} fusion(f32[96,4096]{1,0:T(8,128)S(1)} %bitcast.298, f32[2,2048,4096]{2,1,0:T(8,128)} %param.5), kind=kOutput, calls=%fused_computation.2 | convolution fusion | flops 9663676416 | bytes 35913728 | tf_op jit(solution)/shard_map/dot_general | solution.py:58
  823.0 36.9 %fusion.10 = f32[96,2048]{1,0:T(8,128)} fusion(f32[96,4096]{1,0:T(8,128)S(1)} %bitcast.299, f32[2,2048,4096]{2,1,0:T(8,128)} %param.5), kind=kOutput, calls=%fused_computation.10 | convolution fusion | flops 9663676416 | bytes 35913728 | tf_op jit(solution)/shard_map/dot_general | solution.py:55
  862.1 22.5 %reduce-scatter.9.cloned.1.call-done = f32[2,48,512]{2,1,0:T(8,128)} async-done(((f32[2,48,2048]{2,1,0:T(8,128)}), f32[2,48,512]{2,1,0:T(8,128)}) %reduce-scatter.9.cloned.1.call-update) | async-done | bytes 196624 | tf_op jit(solution)/shard_map/reduce_scatter | solution.py:79
  885.8 1.2 fusion.85
  888.2 1.2 fusion.35
  889.4 39.9 %psum.58 = f32[2,48,48]{2,1,0:T(8,128)S(1)} all-reduce(f32[2,48,48]{2,1,0:T(8,128)S(1)} %pad_maximum_fusion.11), channel_id=1, replica_groups=mesh['rows'=8,'cols'=4] {'rows','cols'}, use_global_device_ids=true, to_apply=%region_7.10 | all-reduce | flops 4608 | bytes 36864 | tf_op jit(solution)/shard_map/psum | solution.py:80
  931.2 1.7 copy.43
  932.9 1.5 reshape.150
  936.0 8.8 cholesky.96
  946.2 7.4 custom-call.10
  954.7 3.5 stack.166
  958.2 5.4 all-to-all-start.3
  967.7 135.9 %all-to-all-done.3 = f32[32,2,48,512]{3,2,1,0:T(8,128)} async-done(((f32[32,2,48,512]{3,2,1,0:T(8,128)}), f32[32,2,48,512]{3,2,1,0:T(8,128)}, u32[]{:S(2)}, u32[]{:S(2)}) %all-to-all-start.3) | async-done | bytes 6291488 | tf_op jit(solution)/shard_map/all_to_all | solution.py:14
  1103.6 3.5 copy.61
  1107.2 36.2 %fusion = f32[96,2048]{1,0:T(8,128)S(1)} fusion(f32[96,4096]{1,0:T(8,128)S(1)} %bitcast.292, f32[2,2048,4096]{2,1,0:T(8,128)} %param.5), kind=kOutput, calls=%fused_computation | convolution fusion | flops 9663676416 | bytes 35913728 | tf_op jit(solution)/shard_map/dot_general | solution.py:58
  1143.4 36.7 %fusion.8 = f32[96,2048]{1,0:T(8,128)} fusion(f32[96,4096]{1,0:T(8,128)S(1)} %bitcast.293, f32[2,2048,4096]{2,1,0:T(8,128)} %param.5), kind=kOutput, calls=%fused_computation.8 | convolution fusion | flops 9663676416 | bytes 35913728 | tf_op jit(solution)/shard_map/dot_general | solution.py:55
  1180.1 1.2 fusion.41
  1188.5 18.3 %reduce-scatter.11.cloned.1.call-done = f32[2,48,512]{2,1,0:T(8,128)} async-done(((f32[2,48,2048]{2,1,0:T(8,128)}), f32[2,48,512]{2,1,0:T(8,128)}) %reduce-scatter.11.cloned.1.call-update) | async-done | bytes 196624 | tf_op jit(solution)/shard_map/reduce_scatter | solution.py:79
  1213.1 1.2 fusion.87
  1215.5 1.2 fusion.33
  1218.6 126.8 %all-reduce.3.cloned.1.call-done = (f32[2,48,48]{2,1,0:T(8,128)}, f32[2,48,48]{2,1,0:T(8,128)}, f32[2,48,48]{2,1,0:T(8,128)}, f32[2,48,48]{2,1,0:T(8,128)}, f32[2,48,48]{2,1,0:T(8,128)}) async-done(((f32[2,48,48]{2,1,0:T(8,128)}, f32[2,48,48]{2,1,0:T(8,128)}, f32[2,48,48]{2,1,0:T(8,128)}, f32[2,48,48]{2,1,0:T(8,128)}, f32[2,48,48]{2,1,0:T(8,128)}), (f32[2,48,48]{2,1,0:T(8,128)}, f32[2,48,48]{2,1,0:T(8,128)}, ...) | async-done | bytes 92176 | tf_op jit(solution)/shard_map/psum | solution.py:80
  1348.3 8.8 cholesky.107
  1358.4 7.4 custom-call.11
  (145 shorter events, 61.5 us)
Async XLA Ops:
  7.2 1.1 copy-start
  11.8 147.4 %all-to-all-start = ((f32[32,2,48,512]{3,2,1,0:T(8,128)}), f32[32,2,48,512]{3,2,1,0:T(8,128)}, u32[]{:S(2)}, u32[]{:S(2)}) async-start(f32[32,2,48,512]{3,2,1,0:T(8,128)} %stack.130), calls=%async_computation | async-start | bytes 12582912 | tf_op jit(solution)/shard_map/all_to_all | solution.py:14
  19.2 242.9 %reduce-scatter.5.cloned.1.call-start = ((), (), s32[]{:S(2)}) async-start(), calls=%async_computation.8 | async-start | bytes 983040 | tf_op jit(solution)/shard_map/reduce_scatter | solution.py:79
  237.7 334.0 %reduce-scatter.7.cloned.1.call-start = ((), (), s32[]{:S(2)}) async-start(), calls=%async_computation.9 | async-start | bytes 983040 | tf_op jit(solution)/shard_map/reduce_scatter | solution.py:79
  549.1 335.5 %reduce-scatter.9.cloned.1.call-start = ((), (), s32[]{:S(2)}) async-start(), calls=%async_computation.10 | async-start | bytes 983040 | tf_op jit(solution)/shard_map/reduce_scatter | solution.py:79
  641.1 144.8 %copy-start.4 = (f32[48,2,512]{2,1,0:T(2,128)}, f32[48,2,512]{2,1,0:T(2,128)S(1)}, u32[]{:S(2)}) copy-start(f32[48,2,512]{2,1,0:T(2,128)S(1)} %reshape.146) | copy-start | bytes 589828
  954.0 0.7 copy-start.5
  958.2 5.5 copy-start.1
  958.2 7.9 copy-start.2
  958.2 145.4 %all-to-all-start.3 = ((f32[32,2,48,512]{3,2,1,0:T(8,128)}), f32[32,2,48,512]{3,2,1,0:T(8,128)}, u32[]{:S(2)}, u32[]{:S(2)}) async-start(f32[32,2,48,512]{3,2,1,0:T(8,128)} %stack.166), calls=%async_computation.6 | async-start | bytes 12582912 | tf_op jit(solution)/shard_map/all_to_all | solution.py:14
  963.6 243.2 %reduce-scatter.11.cloned.1.call-start = ((), (), s32[]{:S(2)}) async-start(), calls=%async_computation.11 | async-start | bytes 983040 | tf_op jit(solution)/shard_map/reduce_scatter | solution.py:79
  1143.4 43.4 %copy-start.3 = (f32[2,48,512]{2,1,0:T(8,128)S(1)}, f32[2,48,512]{2,1,0:T(8,128)}, u32[]{:S(2)}) copy-start(f32[2,48,512]{2,1,0:T(8,128)} %reduce-scatter.9.cloned.1.call-done) | copy-start | bytes 589828
  1180.1 8.2 copy-start.6
  1182.3 163.1 %all-reduce.3.cloned.1.call-start = ((), (), s32[]{:S(2)}) async-start(), calls=%async_computation.12 | async-start | bytes 491520 | tf_op jit(solution)/shard_map/psum | solution.py:80
  1345.4 22.3 %copy-start.7 = (f32[2,48,48]{2,1,0:T(8,128)S(1)}, f32[2,48,48]{2,1,0:T(8,128)}, u32[]{:S(2)}) copy-start(f32[2,48,48]{2,1,0:T(8,128)} %get-tuple-element.7) | copy-start | bytes 55300
  1345.4 22.4 %copy-start.8 = (f32[2,48,48]{2,1,0:T(8,128)S(1)}, f32[2,48,48]{2,1,0:T(8,128)}, u32[]{:S(2)}) copy-start(f32[2,48,48]{2,1,0:T(8,128)} %get-tuple-element.8) | copy-start | bytes 55300
Sparse Core Ops, SparseCore 0:
  237.8 24.3 reduce-scatter.4
  549.3 22.3 reduce-scatter.6
  862.2 22.3 reduce-scatter.8
  1182.5 24.3 reduce-scatter.10
  1217.5 127.9 all-reduce.2
